TPU v7x, 32 devices: a whole 2x2x4 slice. The times are simulated.
32 devices in a mesh: snap: 4 (over z), param: 8 (over y, x, core).
Axes of the slice: x: 2, y: 2, z: 4, core: 2. Of those that a mesh axis runs over, the one named last changes fastest.
Arguments:
- snapshots: bfloat16 [256, 512, 1024], P('snap', 'param'), as said below
- coeffs: float32 [16, 256], P(None, 'snap'), may hold values from -0.375 to 0.375
Outputs:
- averages: float32 [16, 512, 1024], P(None, 'param', 'snap')
- width_norms: float32 [16], replicated
Inputs may be any that keep to these rules, and one draw needn't show every extreme that they name: `snapshots`: stored snapshot weights, finite.
All inputs are finite; a program needn't handle non-finite values.
Results may differ from a plain program's by a relative error of at most 0.0003.
Values may be sent and summed in bfloat16 or wider, within the bound.
A program may use at most 64 MiB of HBM per device.

v0:
```python
import jax
import jax.numpy as jnp
from jax import lax
from jax.sharding import PartitionSpec as P


def combine(weights, stored):
    flat = stored.reshape(stored.shape[0], stored.shape[1] * stored.shape[2]).astype(jnp.float32)
    product = jnp.dot(
        weights, flat, precision=lax.Precision.HIGHEST, preferred_element_type=jnp.float32
    )
    return product.reshape(weights.shape[0], stored.shape[1], stored.shape[2])


def on_device(snapshots, coeffs):
    partial_value = combine(coeffs, snapshots)
    averages = lax.psum_scatter(partial_value, "snap", scatter_dimension=2, tiled=True)
    squares = jnp.sum(averages * averages, axis=(1, 2))
    total = lax.psum(squares, ("snap", "param"))
    entries = averages.shape[1] * averages.shape[2] * lax.axis_size("snap") * lax.axis_size("param")
    width_norms = jnp.sqrt(total / jnp.float32(entries))
    return (averages, width_norms)


def solution(mesh):
    in_specs = (P("snap", "param", None), P(None, "snap"))
    out_specs = (P(None, "param", "snap"), P())
    return jax.shard_map(
        on_device, mesh=mesh, in_specs=in_specs, out_specs=out_specs, check_vma=False
    )
```

profile of v0, /device:TPU:0, one launch (start us, length us, event | category | flops | bytes accessed | tf_op | source)
XLA Modules:
  0.0 157.1 jit_solution(16905915047605514298)
XLA Ops:
  7.2 0.0 copy-start
  7.2 0.0 reduce-scatter.2.cloned.1.call-start
  7.2 0.6 copy-done
  7.9 17.1 %fusion = f32[16,64,1024]{2,0,1:T(8,128)} fusion(f32[16,64]{1,0:T(8,128)S(1)} %copy-done, bf16[8,8,64,1024]{3,2,1,0:T(8,128)(2,1)} %bitcast.14), kind=kOutput, calls=%fused_computation | convolution fusion | flops 805306368 | bytes 12587008 | tf_op jit(solution)/shard_map/dot_general | solution.py:9
  25.0 0.0 reduce-scatter.2.cloned.1.call-update
  25.0 79.7 %reduce-scatter.2.cloned.1.call-done = f32[16,64,256]{2,0,1:T(8,128)} async-done(((f32[16,64,1024]{2,0,1:T(8,128)}), f32[16,64,256]{2,0,1:T(8,128)}) %reduce-scatter.2.cloned.1.call-update) | async-done | bytes 1048592 | tf_op jit(solution)/shard_map/reduce_scatter | solution.py:17
  104.7 1.5 multiply_reduce_fusion
  106.2 40.7 %psum.7 = f32[16]{0:T(128)S(1)} all-reduce(f32[16]{0:T(128)S(1)} %multiply_reduce_fusion), channel_id=1, replica_groups=mesh['snap'=4,'param'=8] {'snap','param'}, use_global_device_ids=true, to_apply=%region_2.0 | all-reduce | flops 16 | bytes 128 | tf_op jit(solution)/shard_map/psum | solution.py:19
  146.9 0.5 multiply_sqrt_fusion
  147.4 2.8 %copy.6 = f32[16,64,256]{2,1,0:T(8,128)} copy(f32[16,64,256]{2,0,1:T(8,128)} %reduce-scatter.2.cloned.1.call-done) | data formatting | bytes 2097152
Async XLA Ops:
  7.2 0.7 copy-start
  7.2 97.5 %reduce-scatter.2.cloned.1.call-start = ((), (), s32[]{:S(2)}) async-start(), calls=%async_computation.1 | async-start | bytes 5242880 | tf_op jit(solution)/shard_map/reduce_scatter | solution.py:17
Sparse Core Ops, SparseCore 0:
  25.2 79.5 reduce-scatter.1
where the time goes:
time: 157 us
  waiting for transfers between devices  79.7 us (51%)
  blocking collectives  40.7 us (26%)
  matrix products  17.1 us (11%)
  between operations  14 us (9%)
  local copies, waits for them, and re-layouts  3.45 us (2%)
  other arithmetic  1.99 us (1%)
    reduce_scatter x1, waiting for transfers between devices, on_device(): lax.psum_scatter(partial_value, 'snap', scatter_dimension=2, tiled=True)  79.7 us
    psum x1, blocking collectives, on_device(): total = lax.psum(squares, ('snap', 'param'))  40.7 us
    dot_general x1, matrix products, combine(): jnp.dot(weights, flat, precision=lax.Precision.HIGHEST, preferred_element...  17.1 us
    unnamed x3, local copies, waits for them, and re-layouts  3.45 us
  transfers between devices with their start and end apart: 1, of which 1 were waited for; matrix products, arithmetic and copies ran while one was open for 0% of the time, Pallas kernels for 0%

commit v1 on v0

v1 whole, which is shorter than its diff:
```python
import functools

import jax
import jax.numpy as jnp
from jax import lax
from jax.experimental import pallas as pl
from jax.experimental.pallas import tpu as pltpu
from jax.sharding import PartitionSpec as P

MESH = pl.DeviceIdType.MESH
GROUP = 16
LAG = 2
POWER = 15
TOP = 2.0**8.375


def encode(value):
    largest = jnp.max(jnp.max(jnp.abs(value), axis=0), axis=0, keepdims=True)
    largest = jnp.maximum(largest, 1e-30)
    x = value * (TOP / largest)[None]
    x2 = x * x
    x4 = x2 * x2
    x8 = x4 * x4
    return ((x8 * x4) * (x2 * x)).astype(jnp.bfloat16), largest * (1.0 / TOP)


def decode(code, scale):
    y = code.astype(jnp.float32)
    size = jnp.exp2(jnp.log2(jnp.maximum(jnp.abs(y), 1e-38)) * (1.0 / POWER)) * scale[None]
    return jnp.where(y > 0.0, size, jnp.where(y < 0.0, -size, 0.0))


def kernel(
    n, peers, entries, coeffs, stored, averages, norms,
    spread, tiles, part, out_code, out_scale, in_code, in_scale, rows, planes,
    load_sem, send_sem, send_scale_sem, recv_sem, recv_scale_sem,
    row_send, row_recv, plane_send, plane_recv,
):
    z = lax.axis_index("snap")
    me = lax.axis_index("param")
    widths, count = coeffs.shape
    keep = stored.shape[2] // n
    groups = stored.shape[1] // GROUP
    steps = (n - 1) * groups
    low = z < n // 2

    barrier = pltpu.get_barrier_semaphore()
    for k in range(1, n):
        pl.semaphore_signal(barrier, inc=1, device_id={"snap": lax.rem(z + k, n)}, device_id_type=MESH)

    @pl.loop(1, peers)
    def _(k):
        pl.semaphore_signal(barrier, inc=1, device_id={"param": lax.rem(me + k, peers)}, device_id_type=MESH)

    def load(i):
        q, t = i // groups, lax.rem(i, groups)
        d = jnp.where(low, n - 1 - q, q)
        return pltpu.make_async_copy(
            stored.at[:, pl.ds(pl.multiple_of(t * GROUP, GROUP), GROUP), pl.ds(pl.multiple_of(d * keep, keep), keep)],
            tiles.at[i],
            load_sem.at[i],
        )

    @pl.loop(0, n * groups)
    def _(i):
        load(i).start()

    exact = coeffs[...]
    high = exact.astype(jnp.bfloat16)
    rest = (exact - high.astype(jnp.float32)).astype(jnp.bfloat16)
    both = jnp.concatenate([high, rest], axis=0)
    tall, wide = spread.shape
    row = lax.broadcasted_iota(jnp.int32, (tall, 2 * widths), 0)
    col = lax.broadcasted_iota(jnp.int32, (tall, 2 * widths), 1)
    pick = jnp.where(row // GROUP == col, 1.0, 0.0).astype(jnp.bfloat16)
    row = lax.broadcasted_iota(jnp.int32, (count, wide), 0)
    col = lax.broadcasted_iota(jnp.int32, (count, wide), 1)
    repeat = jnp.where(col // GROUP == row, 1.0, 0.0).astype(jnp.bfloat16)
    tall_rows = jnp.dot(pick, both, preferred_element_type=jnp.float32).astype(jnp.bfloat16)
    full = jnp.dot(tall_rows, repeat, preferred_element_type=jnp.float32)
    row = lax.broadcasted_iota(jnp.int32, (tall, wide), 0)
    col = lax.broadcasted_iota(jnp.int32, (tall, wide), 1)
    spread[...] = jnp.where(row % GROUP == col % GROUP, full, 0.0).astype(jnp.bfloat16)

    pl.semaphore_wait(barrier, n - 1 + peers - 1)

    def copies(way, k, peer):
        code = pltpu.make_async_remote_copy(
            src_ref=out_code.at[way, k], dst_ref=in_code.at[way, k],
            send_sem=send_sem.at[way, k], recv_sem=recv_sem.at[way, k],
            device_id={"snap": peer}, device_id_type=MESH,
        )
        scale = pltpu.make_async_remote_copy(
            src_ref=out_scale.at[way, k], dst_ref=in_scale.at[way, k],
            send_sem=send_scale_sem.at[way, k], recv_sem=recv_scale_sem.at[way, k],
            device_id={"snap": peer}, device_id_type=MESH,
        )
        return scale, code

    def send(way, k, peer, value):
        code, scale = encode(value)
        out_code[way, k] = code
        out_scale[way, k] = scale
        for copy in copies(way, k, peer):
            copy.start()

    half = widths * GROUP

    @pl.loop(0, n * groups)
    def _(i):
        q, t = i // groups, lax.rem(i, groups)
        d = jnp.where(low, n - 1 - q, q)
        load(i).wait()
        both_parts = jnp.dot(
            spread[...], tiles[i].reshape(count * GROUP, keep), preferred_element_type=jnp.float32
        )
        value = (both_parts[:half] + both_parts[half:]).reshape(widths, GROUP, keep)
        part[d, t] = value

        @pl.when(jnp.logical_and(jnp.logical_or(z == 0, z == n - 1), d != z))
        def _():
            way = jnp.where(z == 0, 0, 1)
            peer = jnp.where(z == 0, 1, n - 2)
            send(way, i, peer, value)

    def pass_on(way, k, d, peer):
        t = lax.rem(k, groups)
        for copy in copies(way, k, peer):
            copy.wait_recv()
        value = part[d, t] + decode(in_code[way, k], in_scale[way, k])

        @pl.when(d == z)
        def _():
            part[d, t] = value

        @pl.when(d != z)
        def _():
            send(way, k, peer, value)

    @pl.loop(0, steps)
    def _(j):
        up = j - LAG * (z - 1)

        @pl.when(jnp.logical_and(z > 0, jnp.logical_and(up >= 0, up < (n - z) * groups)))
        def _():
            pass_on(0, up, n - 1 - up // groups, jnp.where(z == n - 1, z - 1, z + 1))

        down = j - LAG * (n - 2 - z)

        @pl.when(jnp.logical_and(z < n - 1, jnp.logical_and(down >= 0, down < (z + 1) * groups)))
        def _():
            pass_on(1, down, down // groups, jnp.where(z == 0, z + 1, z - 1))

    sums = jnp.zeros((widths, 1), jnp.float32)
    for t in range(groups):
        value = part[z, t]
        averages[:, t * GROUP : (t + 1) * GROUP, :] = value
        sums += jnp.sum(jnp.sum(value * value, axis=1), axis=1, keepdims=True)
    lanes = norms.shape[1]
    row = lax.broadcasted_iota(jnp.int32, (widths, lanes), 0)
    col = lax.broadcasted_iota(jnp.int32, (widths, lanes), 1)
    line = jnp.sum(jnp.where(row == col, sums, 0.0), axis=0, keepdims=True)

    def share(buffer, sends, recvs, axis, mine, size, value):
        buffer[mine] = value

        def copy(k, slot):
            return pltpu.make_async_remote_copy(
                src_ref=buffer.at[slot], dst_ref=buffer.at[slot],
                send_sem=sends.at[k], recv_sem=recvs.at[slot],
                device_id={axis: lax.rem(mine + k, size)}, device_id_type=MESH,
            )

        @pl.loop(1, size)
        def _(k):
            copy(k, mine).start()

        @pl.loop(1, size)
        def _(k):
            copy(k, lax.rem(mine + k, size)).wait_recv()

        @pl.loop(1, size)
        def _(k):
            copy(k, mine).wait_send()

        return jnp.sum(buffer[...], axis=0)

    line = share(rows, row_send, row_recv, "param", me, peers, line)
    line = share(planes, plane_send, plane_recv, "snap", z, n, line)
    norms[...] = jnp.sqrt(line / jnp.float32(entries))

    @pl.loop(0, steps)
    def _(k):
        @pl.when(k < (n - 1 - z) * groups)
        def _():
            for copy in copies(0, k, jnp.where(z == n - 1, z - 1, z + 1)):
                copy.wait_send()

        @pl.when(k < z * groups)
        def _():
            for copy in copies(1, k, jnp.where(z == 0, z + 1, z - 1)):
                copy.wait_send()


def on_device(n, peers, snapshots, coeffs):
    count, height, cols = snapshots.shape
    widths = coeffs.shape[0]
    keep = cols // n
    groups = height // GROUP
    steps = (n - 1) * groups
    entries = height * cols * peers
    dma = pltpu.SemaphoreType.DMA
    averages, norms = pl.pallas_call(
        functools.partial(kernel, n, peers, entries),
        out_shape=(
            jax.ShapeDtypeStruct((widths, height, keep), jnp.float32),
            jax.ShapeDtypeStruct((1, 128), jnp.float32),
        ),
        in_specs=[pl.BlockSpec(memory_space=pltpu.VMEM), pl.BlockSpec(memory_space=pl.ANY)],
        out_specs=(pl.BlockSpec(memory_space=pltpu.VMEM), pl.BlockSpec(memory_space=pltpu.VMEM)),
        scratch_shapes=[
            pltpu.VMEM((2 * widths * GROUP, count * GROUP), jnp.bfloat16),
            pltpu.VMEM((n * groups, count, GROUP, keep), jnp.bfloat16),
            pltpu.VMEM((n, groups, widths, GROUP, keep), jnp.float32),
            pltpu.VMEM((2, steps, widths, GROUP, keep), jnp.bfloat16),
            pltpu.VMEM((2, steps, 1, keep), jnp.float32),
            pltpu.VMEM((2, steps, widths, GROUP, keep), jnp.bfloat16),
            pltpu.VMEM((2, steps, 1, keep), jnp.float32),
            pltpu.VMEM((peers, 1, 128), jnp.float32),
            pltpu.VMEM((n, 1, 128), jnp.float32),
            dma((n * groups,)),
            dma((2, steps)), dma((2, steps)), dma((2, steps)), dma((2, steps)),
            dma((peers,)), dma((peers,)), dma((n,)), dma((n,)),
        ],
        compiler_params=pltpu.CompilerParams(
            collective_id=0, has_side_effects=True, vmem_limit_bytes=48 * 1024 * 1024
        ),
        name="reconstruct",
    )(coeffs, snapshots)
    return averages, norms[0, :widths]


def solution(mesh):
    in_specs = (P("snap", "param", None), P(None, "snap"))
    out_specs = (P(None, "param", "snap"), P())
    body = functools.partial(on_device, mesh.shape["snap"], mesh.shape["param"])
    return jax.shard_map(body, mesh=mesh, in_specs=in_specs, out_specs=out_specs, check_vma=False)
```

time: 157 us -> 52.5 us (0.33)
  waiting for transfers between devices: 79.7 us -> 0 us
  Pallas kernels: 0 us -> 49.5 us
  blocking collectives: 40.7 us -> 0 us
  matrix products: 17.1 us -> 0 us
  between operations: 14 us -> 0.65 us
  other arithmetic: 1.99 us -> 0 us
    reduce_scatter x1 -> x0, waiting for transfers between devices: 79.7 us -> none  [on_device(): lax.psum_scatter(partial_value, 'snap', scatter_dimension=2, tiled=True)]
    pallas_call x0 -> x1, Pallas kernels: none -> 49.5 us  [on_device(): pl.pallas_call(functools.partial(kernel, n, peers, entries), out_shape=(j...]
    psum x1 -> x0, blocking collectives: 40.7 us -> none  [on_device(): total = lax.psum(squares, ('snap', 'param'))]
    dot_general x1 -> x0, matrix products: 17.1 us -> none  [combine(): jnp.dot(weights, flat, precision=lax.Precision.HIGHEST, preferred_element...]
    unnamed x3, local copies, waits for them, and re-layouts: 3.45 us -> 1.66 us
  transfers between devices with their start and end apart: 1 -> 0, of which waited for: 1 -> 0; matrix products, arithmetic and copies ran while one was open for 0% -> 0% of each run, Pallas kernels for 0% -> 0%
where the time goes in v1:
time: 52.5 us; the launch traced here: 52.3 us
  Pallas kernels  49.5 us (94%)
  local copies, waits for them, and re-layouts  2.17 us (4%)
  between operations  0.65 us (1%)
    pallas_call x1, Pallas kernels, on_device(): pl.pallas_call(functools.partial(kernel, n, peers, entries), out_shape=(j...  49.5 us
    unnamed x3, local copies, waits for them, and re-layouts  1.66 us

profile of v1, /device:TPU:0, one launch (start us, length us, event | category | flops | bytes accessed | tf_op | source)
XLA Modules:
  0.0 52.3 jit_solution(4780513220934491932)
XLA Ops:
  0.6 0.0 copy-start
  0.6 0.7 %copy-done = f32[16,64]{1,0:T(8,128)S(1)} copy-done((f32[16,64]{1,0:T(8,128)S(1)}, f32[16,64]{1,0:T(8,128)}, u32[]{:S(2)}) %copy-start) | copy-done | bytes 4120
  1.3 49.5 %reconstruct.1 = (f32[16,64,256]{2,1,0:T(8,128)S(1)}, f32[1,128]{1,0:T(1,128)S(1)}) custom-call(f32[16,64]{1,0:T(8,128)S(1)} %copy-done, bf16[64,64,1024]{2,1,0:T(8,128)(2,1)} %stored.1), custom_call_target="tpu_custom_call" | custom-call | tf_op jit(solution)/shard_map/reconstruct/pallas_call | solution.py:213
  50.8 0.5 slice_bitcast_fusion
  51.3 1.0 %copy.5 = f32[16,64,256]{2,1,0:T(8,128)} copy(f32[16,64,256]{2,1,0:T(8,128)S(1)} %get-tuple-element.8) | data formatting | bytes 2097152
Async XLA Ops:
  0.6 0.7 %copy-start = (f32[16,64]{1,0:T(8,128)S(1)}, f32[16,64]{1,0:T(8,128)}, u32[]{:S(2)}) copy-start(f32[16,64]{1,0:T(8,128)} %coeffs.1) | copy-start | bytes 12292

commit v2 on v1

--- a/solution.py
+++ b/solution.py
@@ -9,8 +9,9 @@
 
 MESH = pl.DeviceIdType.MESH
 GROUP = 16
-LAG = 2
+LAG = 3
 POWER = 15
+AHEAD = 4
 TOP = 2.0**8.375
 
 
@@ -32,9 +33,9 @@
 
 def kernel(
     n, peers, entries, coeffs, stored, averages, norms,
-    spread, tiles, part, out_code, out_scale, in_code, in_scale, rows, planes,
-    load_sem, send_sem, send_scale_sem, recv_sem, recv_scale_sem,
-    row_send, row_recv, plane_send, plane_recv,
+    exact, spread, tiles, part, out_code, out_scale, in_code, in_scale, squares, lines,
+    exact_sem, load_sem, send_sem, send_scale_sem, recv_sem, recv_scale_sem,
+    line_send, line_recv, known,
 ):
     z = lax.axis_index("snap")
     me = lax.axis_index("param")
@@ -42,6 +43,7 @@
     keep = stored.shape[2] // n
     groups = stored.shape[1] // GROUP
     steps = (n - 1) * groups
+    lag = min(LAG, groups - 1)
     low = z < n // 2
 
     barrier = pltpu.get_barrier_semaphore()
@@ -61,13 +63,15 @@
             load_sem.at[i],
         )
 
-    @pl.loop(0, n * groups)
-    def _(i):
+    fetch = pltpu.make_async_copy(coeffs, exact, exact_sem)
+    fetch.start()
+    for i in range(min(AHEAD, n * groups)):
         load(i).start()
-
-    exact = coeffs[...]
-    high = exact.astype(jnp.bfloat16)
-    rest = (exact - high.astype(jnp.float32)).astype(jnp.bfloat16)
+    fetch.wait()
+
+    whole = exact[...]
+    high = whole.astype(jnp.bfloat16)
+    rest = (whole - high.astype(jnp.float32)).astype(jnp.bfloat16)
     both = jnp.concatenate([high, rest], axis=0)
     tall, wide = spread.shape
     row = lax.broadcasted_iota(jnp.int32, (tall, 2 * widths), 0)
@@ -78,11 +82,11 @@
     repeat = jnp.where(col // GROUP == row, 1.0, 0.0).astype(jnp.bfloat16)
     tall_rows = jnp.dot(pick, both, preferred_element_type=jnp.float32).astype(jnp.bfloat16)
     full = jnp.dot(tall_rows, repeat, preferred_element_type=jnp.float32)
-    row = lax.broadcasted_iota(jnp.int32, (tall, wide), 0)
-    col = lax.broadcasted_iota(jnp.int32, (tall, wide), 1)
-    spread[...] = jnp.where(row % GROUP == col % GROUP, full, 0.0).astype(jnp.bfloat16)
-
-    pl.semaphore_wait(barrier, n - 1 + peers - 1)
+    row = lax.broadcasted_iota(jnp.int32, (GROUP, wide), 0)
+    col = lax.broadcasted_iota(jnp.int32, (GROUP, wide), 1)
+    same = (row == col % GROUP)[None]
+    full = jnp.where(same, full.reshape(2 * widths, GROUP, wide), 0.0)
+    spread[...] = full.reshape(tall, wide).astype(jnp.bfloat16)
 
     def copies(way, k, peer):
         code = pltpu.make_async_remote_copy(
@@ -111,17 +115,32 @@
         q, t = i // groups, lax.rem(i, groups)
         d = jnp.where(low, n - 1 - q, q)
         load(i).wait()
+
+        @pl.when(i + AHEAD < n * groups)
+        def _():
+            load(i + AHEAD).start()
+
         both_parts = jnp.dot(
             spread[...], tiles[i].reshape(count * GROUP, keep), preferred_element_type=jnp.float32
         )
         value = (both_parts[:half] + both_parts[half:]).reshape(widths, GROUP, keep)
         part[d, t] = value
+
+        @pl.when(i == 0)
+        def _():
+            pl.semaphore_wait(barrier, n - 1 + peers - 1)
 
         @pl.when(jnp.logical_and(jnp.logical_or(z == 0, z == n - 1), d != z))
         def _():
             way = jnp.where(z == 0, 0, 1)
             peer = jnp.where(z == 0, 1, n - 2)
             send(way, i, peer, value)
+
+    @pl.loop(1, peers)
+    def _(k):
+        pl.semaphore_signal(known, inc=1, device_id={"param": lax.rem(me + k, peers)}, device_id_type=MESH)
+
+    last = jnp.where(jnp.logical_or(jnp.logical_and(z > 0, 2 * z < n - 1), z == n - 1), 0, 1)
 
     def pass_on(way, k, d, peer):
         t = lax.rem(k, groups)
@@ -131,7 +150,14 @@
 
         @pl.when(d == z)
         def _():
-            part[d, t] = value
+            @pl.when(way != last)
+            def _():
+                part[d, t] = value
+
+            @pl.when(way == last)
+            def _():
+                averages[:, pl.ds(pl.multiple_of(t * GROUP, GROUP), GROUP), :] = value
+                squares[t] = jnp.sum(value * value, axis=1)
 
         @pl.when(d != z)
         def _():
@@ -139,55 +165,59 @@
 
     @pl.loop(0, steps)
     def _(j):
-        up = j - LAG * (z - 1)
+        up = j - lag * (z - 1)
 
         @pl.when(jnp.logical_and(z > 0, jnp.logical_and(up >= 0, up < (n - z) * groups)))
         def _():
             pass_on(0, up, n - 1 - up // groups, jnp.where(z == n - 1, z - 1, z + 1))
 
-        down = j - LAG * (n - 2 - z)
+        down = j - lag * (n - 2 - z)
 
         @pl.when(jnp.logical_and(z < n - 1, jnp.logical_and(down >= 0, down < (z + 1) * groups)))
         def _():
             pass_on(1, down, down // groups, jnp.where(z == 0, z + 1, z - 1))
 
-    sums = jnp.zeros((widths, 1), jnp.float32)
-    for t in range(groups):
-        value = part[z, t]
-        averages[:, t * GROUP : (t + 1) * GROUP, :] = value
-        sums += jnp.sum(jnp.sum(value * value, axis=1), axis=1, keepdims=True)
+    sums = jnp.sum(jnp.sum(squares[...], axis=0), axis=1, keepdims=True)
     lanes = norms.shape[1]
     row = lax.broadcasted_iota(jnp.int32, (widths, lanes), 0)
     col = lax.broadcasted_iota(jnp.int32, (widths, lanes), 1)
     line = jnp.sum(jnp.where(row == col, sums, 0.0), axis=0, keepdims=True)
 
-    def share(buffer, sends, recvs, axis, mine, size, value):
-        buffer[mine] = value
-
-        def copy(k, slot):
-            return pltpu.make_async_remote_copy(
-                src_ref=buffer.at[slot], dst_ref=buffer.at[slot],
-                send_sem=sends.at[k], recv_sem=recvs.at[slot],
-                device_id={axis: lax.rem(mine + k, size)}, device_id_type=MESH,
-            )
-
-        @pl.loop(1, size)
+    lines[z * peers + me] = line
+    pl.semaphore_wait(known, peers - 1)
+
+    def tell(j, k):
+        place, peer = lax.rem(z + j, n), lax.rem(me + k, peers)
+        return pltpu.make_async_remote_copy(
+            src_ref=lines.at[z * peers + me], dst_ref=lines.at[z * peers + me],
+            send_sem=line_send.at[j * peers + k], recv_sem=line_recv.at[z * peers + me],
+            device_id={"snap": place, "param": peer}, device_id_type=MESH,
+        )
+
+    def hear(j, k):
+        slot = lax.rem(z + j, n) * peers + lax.rem(me + k, peers)
+        return pltpu.make_async_remote_copy(
+            src_ref=lines.at[slot], dst_ref=lines.at[slot],
+            send_sem=line_send.at[j * peers + k], recv_sem=line_recv.at[slot],
+            device_id={"snap": lax.rem(z + j, n), "param": lax.rem(me + k, peers)}, device_id_type=MESH,
+        )
+
+    for j in range(n):
+        @pl.loop(0 if j else 1, peers)
         def _(k):
-            copy(k, mine).start()
-
-        @pl.loop(1, size)
+            tell(j, k).start()
+
+    for j in range(n):
+        @pl.loop(0 if j else 1, peers)
         def _(k):
-            copy(k, lax.rem(mine + k, size)).wait_recv()
-
-        @pl.loop(1, size)
+            hear(j, k).wait_recv()
+
+    norms[...] = jnp.sqrt(jnp.sum(lines[...], axis=0) / jnp.float32(entries))
+
+    for j in range(n):
+        @pl.loop(0 if j else 1, peers)
         def _(k):
-            copy(k, mine).wait_send()
-
-        return jnp.sum(buffer[...], axis=0)
-
-    line = share(rows, row_send, row_recv, "param", me, peers, line)
-    line = share(planes, plane_send, plane_recv, "snap", z, n, line)
-    norms[...] = jnp.sqrt(line / jnp.float32(entries))
+            tell(j, k).wait_send()
 
     @pl.loop(0, steps)
     def _(k):
@@ -216,9 +246,10 @@
             jax.ShapeDtypeStruct((widths, height, keep), jnp.float32),
             jax.ShapeDtypeStruct((1, 128), jnp.float32),
         ),
-        in_specs=[pl.BlockSpec(memory_space=pltpu.VMEM), pl.BlockSpec(memory_space=pl.ANY)],
+        in_specs=[pl.BlockSpec(memory_space=pltpu.HBM)] * 2,
         out_specs=(pl.BlockSpec(memory_space=pltpu.VMEM), pl.BlockSpec(memory_space=pltpu.VMEM)),
         scratch_shapes=[
+            pltpu.VMEM((widths, count), jnp.float32),
             pltpu.VMEM((2 * widths * GROUP, count * GROUP), jnp.bfloat16),
             pltpu.VMEM((n * groups, count, GROUP, keep), jnp.bfloat16),
             pltpu.VMEM((n, groups, widths, GROUP, keep), jnp.float32),
@@ -226,11 +257,12 @@
             pltpu.VMEM((2, steps, 1, keep), jnp.float32),
             pltpu.VMEM((2, steps, widths, GROUP, keep), jnp.bfloat16),
             pltpu.VMEM((2, steps, 1, keep), jnp.float32),
-            pltpu.VMEM((peers, 1, 128), jnp.float32),
-            pltpu.VMEM((n, 1, 128), jnp.float32),
+            pltpu.VMEM((groups, widths, keep), jnp.float32),
+            pltpu.VMEM((n * peers, 1, 128), jnp.float32),
+            dma(()),
             dma((n * groups,)),
             dma((2, steps)), dma((2, steps)), dma((2, steps)), dma((2, steps)),
-            dma((peers,)), dma((peers,)), dma((n,)), dma((n,)),
+            dma((n * peers,)), dma((n * peers,)), pltpu.SemaphoreType.REGULAR,
         ],
         compiler_params=pltpu.CompilerParams(
             collective_id=0, has_side_effects=True, vmem_limit_bytes=48 * 1024 * 1024

time: 52.5 us -> 50.9 us (0.970)
  Pallas kernels: 49.5 us -> 47.9 us
    pallas_call x1, Pallas kernels: 49.5 us -> 47.9 us  [on_device(): pl.pallas_call(functools.partial(kernel, n, peers, entries), out_shape=(j...]
where the time goes in v2:
time: 50.9 us; the launch traced here: 50.7 us
  Pallas kernels  47.9 us (94%)
  local copies, waits for them, and re-layouts  2.17 us (4%)
  between operations  0.65 us (1%)
    pallas_call x1, Pallas kernels, on_device(): pl.pallas_call(functools.partial(kernel, n, peers, entries), out_shape=(j...  47.9 us
    unnamed x3, local copies, waits for them, and re-layouts  1.66 us

profile of v2, /device:TPU:0, one launch (start us, length us, event | category | flops | bytes accessed | tf_op | source)
XLA Modules:
  0.0 50.7 jit_solution(8047812037631570919)
XLA Ops:
  0.6 0.0 copy-start
  0.6 0.7 %copy-done = f32[16,64]{1,0:T(8,128)S(1)} copy-done((f32[16,64]{1,0:T(8,128)S(1)}, f32[16,64]{1,0:T(8,128)}, u32[]{:S(2)}) %copy-start) | copy-done | bytes 4120
  1.3 47.9 %reconstruct.1 = (f32[16,64,256]{2,1,0:T(8,128)S(1)}, f32[1,128]{1,0:T(1,128)S(1)}) custom-call(f32[16,64]{1,0:T(8,128)S(1)} %copy-done, bf16[64,64,1024]{2,1,0:T(8,128)(2,1)} %stored.1), custom_call_target="tpu_custom_call" | custom-call | tf_op jit(solution)/shard_map/reconstruct/pallas_call | solution.py:243
  49.3 0.5 %slice_bitcast_fusion = f32[16]{0:T(128)} fusion(f32[1,128]{1,0:T(1,128)S(1)} %get-tuple-element.5), kind=kLoop, calls=%fused_computation | loop fusion | bytes 128 | tf_op jit(solution)/shard_map/squeeze | solution.py:272
  49.8 1.0 %copy.5 = f32[16,64,256]{2,1,0:T(8,128)} copy(f32[16,64,256]{2,1,0:T(8,128)S(1)} %get-tuple-element.8) | data formatting | bytes 2097152
Async XLA Ops:
  0.6 0.7 %copy-start = (f32[16,64]{1,0:T(8,128)S(1)}, f32[16,64]{1,0:T(8,128)}, u32[]{:S(2)}) copy-start(f32[16,64]{1,0:T(8,128)} %coeffs.1) | copy-start | bytes 12292

commit v3 on v2

--- a/solution.py
+++ b/solution.py
@@ -31,10 +31,18 @@
     return jnp.where(y > 0.0, size, jnp.where(y < 0.0, -size, 0.0))
 
 
+def each(size, body):
+    if size <= 8:
+        for k in range(size):
+            body(k)
+    else:
+        pl.loop(0, size)(body)
+
+
 def kernel(
     n, peers, entries, coeffs, stored, averages, norms,
-    exact, spread, tiles, part, out_code, out_scale, in_code, in_scale, squares, lines,
-    exact_sem, load_sem, send_sem, send_scale_sem, recv_sem, recv_scale_sem,
+    spread, tiles, part, out_code, out_scale, in_code, in_scale, squares, lines,
+    load_sem, send_sem, send_scale_sem, recv_sem, recv_scale_sem,
     line_send, line_recv, known,
 ):
     z = lax.axis_index("snap")
@@ -46,14 +54,6 @@
     lag = min(LAG, groups - 1)
     low = z < n // 2
 
-    barrier = pltpu.get_barrier_semaphore()
-    for k in range(1, n):
-        pl.semaphore_signal(barrier, inc=1, device_id={"snap": lax.rem(z + k, n)}, device_id_type=MESH)
-
-    @pl.loop(1, peers)
-    def _(k):
-        pl.semaphore_signal(barrier, inc=1, device_id={"param": lax.rem(me + k, peers)}, device_id_type=MESH)
-
     def load(i):
         q, t = i // groups, lax.rem(i, groups)
         d = jnp.where(low, n - 1 - q, q)
@@ -63,13 +63,23 @@
             load_sem.at[i],
         )
 
-    fetch = pltpu.make_async_copy(coeffs, exact, exact_sem)
-    fetch.start()
-    for i in range(min(AHEAD, n * groups)):
+    load(0).start()
+    barrier = pltpu.get_barrier_semaphore()
+
+    def greet(axis, mine):
+        def body(k):
+            @pl.when(k != mine)
+            def _():
+                pl.semaphore_signal(barrier, inc=1, device_id={axis: k}, device_id_type=MESH)
+
+        return body
+
+    each(n, greet("snap", z))
+    each(peers, greet("param", me))
+    for i in range(1, min(AHEAD, n * groups)):
         load(i).start()
-    fetch.wait()
-
-    whole = exact[...]
+
+    whole = coeffs[...]
     high = whole.astype(jnp.bfloat16)
     rest = (whole - high.astype(jnp.float32)).astype(jnp.bfloat16)
     both = jnp.concatenate([high, rest], axis=0)
@@ -136,9 +146,12 @@
             peer = jnp.where(z == 0, 1, n - 2)
             send(way, i, peer, value)
 
-    @pl.loop(1, peers)
-    def _(k):
-        pl.semaphore_signal(known, inc=1, device_id={"param": lax.rem(me + k, peers)}, device_id_type=MESH)
+    def inform(k):
+        @pl.when(k != me)
+        def _():
+            pl.semaphore_signal(known, inc=1, device_id={"param": k}, device_id_type=MESH)
+
+    each(peers, inform)
 
     last = jnp.where(jnp.logical_or(jnp.logical_and(z > 0, 2 * z < n - 1), z == n - 1), 0, 1)
 
@@ -183,41 +196,27 @@
     col = lax.broadcasted_iota(jnp.int32, (widths, lanes), 1)
     line = jnp.sum(jnp.where(row == col, sums, 0.0), axis=0, keepdims=True)
 
-    lines[z * peers + me] = line
+    own = z * peers + me
+    lines[own] = line
     pl.semaphore_wait(known, peers - 1)
 
-    def tell(j, k):
-        place, peer = lax.rem(z + j, n), lax.rem(me + k, peers)
-        return pltpu.make_async_remote_copy(
-            src_ref=lines.at[z * peers + me], dst_ref=lines.at[z * peers + me],
-            send_sem=line_send.at[j * peers + k], recv_sem=line_recv.at[z * peers + me],
-            device_id={"snap": place, "param": peer}, device_id_type=MESH,
-        )
-
-    def hear(j, k):
-        slot = lax.rem(z + j, n) * peers + lax.rem(me + k, peers)
+    def others(act):
+        for p in range(n):
+            def body(k, p=p):
+                @pl.when(jnp.logical_or(p != z, k != me))
+                def _():
+                    act(p, k)
+
+            each(peers, body)
+
+    def line_copy(p, k, slot):
         return pltpu.make_async_remote_copy(
             src_ref=lines.at[slot], dst_ref=lines.at[slot],
-            send_sem=line_send.at[j * peers + k], recv_sem=line_recv.at[slot],
-            device_id={"snap": lax.rem(z + j, n), "param": lax.rem(me + k, peers)}, device_id_type=MESH,
-        )
-
-    for j in range(n):
-        @pl.loop(0 if j else 1, peers)
-        def _(k):
-            tell(j, k).start()
-
-    for j in range(n):
-        @pl.loop(0 if j else 1, peers)
-        def _(k):
-            hear(j, k).wait_recv()
-
-    norms[...] = jnp.sqrt(jnp.sum(lines[...], axis=0) / jnp.float32(entries))
-
-    for j in range(n):
-        @pl.loop(0 if j else 1, peers)
-        def _(k):
-            tell(j, k).wait_send()
+            send_sem=line_send.at[p * peers + k], recv_sem=line_recv.at[slot],
+            device_id={"snap": p, "param": k}, device_id_type=MESH,
+        )
+
+    others(lambda p, k: line_copy(p, k, own).start())
 
     @pl.loop(0, steps)
     def _(k):
@@ -230,6 +229,10 @@
         def _():
             for copy in copies(1, k, jnp.where(z == 0, z + 1, z - 1)):
                 copy.wait_send()
+
+    others(lambda p, k: line_copy(p, k, own).wait_send())
+    others(lambda p, k: line_copy(p, k, p * peers + k).wait_recv())
+    norms[...] = jnp.sqrt(jnp.sum(lines[...], axis=0) / jnp.float32(entries))
 
 
 def on_device(n, peers, snapshots, coeffs):
@@ -246,10 +249,9 @@
             jax.ShapeDtypeStruct((widths, height, keep), jnp.float32),
             jax.ShapeDtypeStruct((1, 128), jnp.float32),
         ),
-        in_specs=[pl.BlockSpec(memory_space=pltpu.HBM)] * 2,
+        in_specs=[pl.BlockSpec(memory_space=pltpu.VMEM), pl.BlockSpec(memory_space=pl.ANY)],
         out_specs=(pl.BlockSpec(memory_space=pltpu.VMEM), pl.BlockSpec(memory_space=pltpu.VMEM)),
         scratch_shapes=[
-            pltpu.VMEM((widths, count), jnp.float32),
             pltpu.VMEM((2 * widths * GROUP, count * GROUP), jnp.bfloat16),
             pltpu.VMEM((n * groups, count, GROUP, keep), jnp.bfloat16),
             pltpu.VMEM((n, groups, widths, GROUP, keep), jnp.float32),
@@ -259,7 +261,6 @@
             pltpu.VMEM((2, steps, 1, keep), jnp.float32),
             pltpu.VMEM((groups, widths, keep), jnp.float32),
             pltpu.VMEM((n * peers, 1, 128), jnp.float32),
-            dma(()),
             dma((n * groups,)),
             dma((2, steps)), dma((2, steps)), dma((2, steps)), dma((2, steps)),
             dma((n * peers,)), dma((n * peers,)), pltpu.SemaphoreType.REGULAR,

time: 50.9 us -> 50.4 us (level)
  no operation moved by 1% of the time
where the time goes in v3:
time: 50.4 us; the launch traced here: 50.3 us
  Pallas kernels  47.4 us (94%)
  local copies, waits for them, and re-layouts  2.17 us (4%)
  between operations  0.65 us (1%)
    pallas_call x1, Pallas kernels, on_device(): pl.pallas_call(functools.partial(kernel, n, peers, entries), out_shape=(j...  47.4 us
    unnamed x3, local copies, waits for them, and re-layouts  1.66 us

profile of v3, /device:TPU:0, one launch (start us, length us, event | category | flops | bytes accessed | tf_op | source)
XLA Modules:
  0.0 50.3 jit_solution(13667216421776954838)
XLA Ops:
  0.6 0.0 copy-start
  0.6 0.7 %copy-done = f32[16,64]{1,0:T(8,128)S(1)} copy-done((f32[16,64]{1,0:T(8,128)S(1)}, f32[16,64]{1,0:T(8,128)}, u32[]{:S(2)}) %copy-start) | copy-done | bytes 4120
  1.3 47.4 %reconstruct.1 = (f32[16,64,256]{2,1,0:T(8,128)S(1)}, f32[1,128]{1,0:T(1,128)S(1)}) custom-call(f32[16,64]{1,0:T(8,128)S(1)} %copy-done, bf16[64,64,1024]{2,1,0:T(8,128)(2,1)} %stored.1), custom_call_target="tpu_custom_call" | custom-call | tf_op jit(solution)/shard_map/reconstruct/pallas_call | solution.py:246
  48.8 0.5 %slice_bitcast_fusion = f32[16]{0:T(128)} fusion(f32[1,128]{1,0:T(1,128)S(1)} %get-tuple-element.5), kind=kLoop, calls=%fused_computation | loop fusion | bytes 128 | tf_op jit(solution)/shard_map/squeeze | solution.py:273
  49.3 1.0 %copy.5 = f32[16,64,256]{2,1,0:T(8,128)} copy(f32[16,64,256]{2,1,0:T(8,128)S(1)} %get-tuple-element.8) | data formatting | bytes 2097152
Async XLA Ops:
  0.6 0.7 %copy-start = (f32[16,64]{1,0:T(8,128)S(1)}, f32[16,64]{1,0:T(8,128)}, u32[]{:S(2)}) copy-start(f32[16,64]{1,0:T(8,128)} %coeffs.1) | copy-start | bytes 12292

commit v4 on v3

--- a/solution.py
+++ b/solution.py
@@ -39,11 +39,20 @@
         pl.loop(0, size)(body)
 
 
+def serves(p, n):
+    return jnp.logical_and(p + 1 <= n - 2, 2 * (p + 1) < n - 1), jnp.logical_and(p - 1 >= 1, 2 * (p - 1) >= n - 1)
+
+
+def has_line(p, n):
+    return p in (0, n - 1) or 2 * (p + 1) < n - 1 or 2 * (p - 1) >= n - 1
+
+
 def kernel(
     n, peers, entries, coeffs, stored, averages, norms,
-    spread, tiles, part, out_code, out_scale, in_code, in_scale, squares, lines,
+    spread, tiles, part, out_code, out_scale, in_code, in_scale,
+    back_out, back_out_scale, back_in, back_in_scale, squares, lines,
     load_sem, send_sem, send_scale_sem, recv_sem, recv_scale_sem,
-    line_send, line_recv, known,
+    back_sem, back_scale_sem, back_recv, back_recv_scale, line_send, line_recv, known,
 ):
     z = lax.axis_index("snap")
     me = lax.axis_index("param")
@@ -64,6 +73,7 @@
         )
 
     load(0).start()
+    squares[...] = jnp.zeros_like(squares)
     barrier = pltpu.get_barrier_semaphore()
 
     def greet(axis, mine):
@@ -155,6 +165,24 @@
 
     last = jnp.where(jnp.logical_or(jnp.logical_and(z > 0, 2 * z < n - 1), z == n - 1), 0, 1)
 
+    inner = jnp.logical_and(z > 0, z < n - 1)
+    above, below = serves(z, n)
+
+    def back_copies(t, peer):
+        code = pltpu.make_async_remote_copy(
+            src_ref=back_out.at[t], dst_ref=back_in.at[t],
+            send_sem=back_sem.at[t], recv_sem=back_recv.at[t],
+            device_id={"snap": peer}, device_id_type=MESH,
+        )
+        scale = pltpu.make_async_remote_copy(
+            src_ref=back_out_scale.at[t], dst_ref=back_in_scale.at[t],
+            send_sem=back_scale_sem.at[t], recv_sem=back_recv_scale.at[t],
+            device_id={"snap": peer}, device_id_type=MESH,
+        )
+        return scale, code
+
+    outward = jnp.where(jnp.logical_and(inner, last == 0), z - 1, jnp.where(inner, z + 1, jnp.where(z == 0, 1, n - 2)))
+
     def pass_on(way, k, d, peer):
         t = lax.rem(k, groups)
         for copy in copies(way, k, peer):
@@ -166,14 +194,23 @@
             @pl.when(way != last)
             def _():
                 part[d, t] = value
+                code, scale = encode(value)
+                back_out[t] = code
+                back_out_scale[t] = scale
+                for copy in back_copies(t, outward):
+                    copy.start()
 
             @pl.when(way == last)
             def _():
                 averages[:, pl.ds(pl.multiple_of(t * GROUP, GROUP), GROUP), :] = value
-                squares[t] = jnp.sum(value * value, axis=1)
+
+                @pl.when(jnp.logical_not(inner))
+                def _():
+                    squares[t] = jnp.sum(value * value, axis=1)
 
         @pl.when(d != z)
         def _():
+            part[d, t] = value
             send(way, k, peer, value)
 
     @pl.loop(0, steps)
@@ -189,6 +226,17 @@
         @pl.when(jnp.logical_and(z < n - 1, jnp.logical_and(down >= 0, down < (z + 1) * groups)))
         def _():
             pass_on(1, down, down // groups, jnp.where(z == 0, z + 1, z - 1))
+
+    @pl.when(jnp.logical_or(above, below))
+    def _():
+        served = jnp.where(above, z + 1, z - 1)
+
+        @pl.loop(0, groups)
+        def _(t):
+            for copy in back_copies(t, served):
+                copy.wait_recv()
+            value = part[served, t] + decode(back_in[t], back_in_scale[t])
+            squares[groups + t] = jnp.sum(value * value, axis=1)
 
     sums = jnp.sum(jnp.sum(squares[...], axis=0), axis=1, keepdims=True)
     lanes = norms.shape[1]
@@ -200,14 +248,17 @@
     lines[own] = line
     pl.semaphore_wait(known, peers - 1)
 
-    def others(act):
-        for p in range(n):
+    def others(act, places):
+        for p in places:
             def body(k, p=p):
                 @pl.when(jnp.logical_or(p != z, k != me))
                 def _():
                     act(p, k)
 
             each(peers, body)
+
+    tellers = [p for p in range(n) if has_line(p, n)]
+    tells = functools.reduce(jnp.logical_or, [z == p for p in tellers])
 
     def line_copy(p, k, slot):
         return pltpu.make_async_remote_copy(
@@ -216,7 +267,10 @@
             device_id={"snap": p, "param": k}, device_id_type=MESH,
         )
 
-    others(lambda p, k: line_copy(p, k, own).start())
+    @pl.when(tells)
+    def _():
+        others(lambda p, k: line_copy(p, k, own).start(), range(n))
+
 
     @pl.loop(0, steps)
     def _(k):
@@ -230,9 +284,22 @@
             for copy in copies(1, k, jnp.where(z == 0, z + 1, z - 1)):
                 copy.wait_send()
 
-    others(lambda p, k: line_copy(p, k, own).wait_send())
-    others(lambda p, k: line_copy(p, k, p * peers + k).wait_recv())
-    norms[...] = jnp.sqrt(jnp.sum(lines[...], axis=0) / jnp.float32(entries))
+    @pl.when(inner)
+    def _():
+        @pl.loop(0, groups)
+        def _(t):
+            for copy in back_copies(t, outward):
+                copy.wait_send()
+
+    @pl.when(tells)
+    def _():
+        others(lambda p, k: line_copy(p, k, own).wait_send(), range(n))
+
+    others(lambda p, k: line_copy(p, k, p * peers + k).wait_recv(), tellers)
+    total = jnp.zeros_like(line)
+    for p in tellers:
+        total += jnp.sum(lines[p * peers : (p + 1) * peers], axis=0)
+    norms[...] = jnp.sqrt(total / jnp.float32(entries))
 
 
 def on_device(n, peers, snapshots, coeffs):
@@ -259,10 +326,15 @@
             pltpu.VMEM((2, steps, 1, keep), jnp.float32),
             pltpu.VMEM((2, steps, widths, GROUP, keep), jnp.bfloat16),
             pltpu.VMEM((2, steps, 1, keep), jnp.float32),
-            pltpu.VMEM((groups, widths, keep), jnp.float32),
+            pltpu.VMEM((groups, widths, GROUP, keep), jnp.bfloat16),
+            pltpu.VMEM((groups, 1, keep), jnp.float32),
+            pltpu.VMEM((groups, widths, GROUP, keep), jnp.bfloat16),
+            pltpu.VMEM((groups, 1, keep), jnp.float32),
+            pltpu.VMEM((2 * groups, widths, keep), jnp.float32),
             pltpu.VMEM((n * peers, 1, 128), jnp.float32),
             dma((n * groups,)),
             dma((2, steps)), dma((2, steps)), dma((2, steps)), dma((2, steps)),
+            dma((groups,)), dma((groups,)), dma((groups,)), dma((groups,)),
             dma((n * peers,)), dma((n * peers,)), pltpu.SemaphoreType.REGULAR,
         ],
         compiler_params=pltpu.CompilerParams(

time: 50.4 us -> 52.6 us (1.044)
  Pallas kernels: 47.4 us -> 49.6 us
    pallas_call x1, Pallas kernels: 47.4 us -> 49.6 us  [on_device(): pl.pallas_call(functools.partial(kernel, n, peers, entries), out_shape=(j...]
where the time goes in v4:
time: 52.6 us; the launch traced here: 52.4 us
  Pallas kernels  49.6 us (94%)
  local copies, waits for them, and re-layouts  2.17 us (4%)
  between operations  0.65 us (1%)
    pallas_call x1, Pallas kernels, on_device(): pl.pallas_call(functools.partial(kernel, n, peers, entries), out_shape=(j...  49.6 us
    unnamed x3, local copies, waits for them, and re-layouts  1.66 us

profile of v4, /device:TPU:0, one launch (start us, length us, event | category | flops | bytes accessed | tf_op | source)
XLA Modules:
  0.0 52.4 jit_solution(12617803268869098695)
XLA Ops:
  0.6 0.0 copy-start
  0.6 0.7 %copy-done = f32[16,64]{1,0:T(8,128)S(1)} copy-done((f32[16,64]{1,0:T(8,128)S(1)}, f32[16,64]{1,0:T(8,128)}, u32[]{:S(2)}) %copy-start) | copy-done | bytes 4120
  1.3 49.6 %reconstruct.1 = (f32[16,64,256]{2,1,0:T(8,128)S(1)}, f32[1,128]{1,0:T(1,128)S(1)}) custom-call(f32[16,64]{1,0:T(8,128)S(1)} %copy-done, bf16[64,64,1024]{2,1,0:T(8,128)(2,1)} %stored.1), custom_call_target="tpu_custom_call" | custom-call | tf_op jit(solution)/shard_map/reconstruct/pallas_call | solution.py:313
  50.9 0.5 slice_bitcast_fusion
  51.4 1.0 %copy.5 = f32[16,64,256]{2,1,0:T(8,128)} copy(f32[16,64,256]{2,1,0:T(8,128)S(1)} %get-tuple-element.8) | data formatting | bytes 2097152
Async XLA Ops:
  0.6 0.7 %copy-start = (f32[16,64]{1,0:T(8,128)S(1)}, f32[16,64]{1,0:T(8,128)}, u32[]{:S(2)}) copy-start(f32[16,64]{1,0:T(8,128)} %coeffs.1) | copy-start | bytes 12292
